TPU v7x, 32 devices: a whole 2x2x4 slice. The times are simulated.
32 devices in a mesh: dev: 8 (over z, y), rep: 4 (over x, core).
Axes of the slice: x: 2, y: 2, z: 4, core: 2. Of those that a mesh axis runs over, the one named last changes fastest.
Arguments:
- features: bfloat16 [32768, 256], P(('dev', 'rep')), may hold values from -6 to 6
- history: bfloat16 [32768, 256], P(('dev', 'rep')), may hold values from -6 to 6
- new_owner: int32 [32, 8], P(('dev', 'rep')), may hold values from 0 to 7, as said below
- pull_rows: int32 [32768], P(('dev', 'rep')), may hold values from 0 to 1023
- occupancy: int32 [256, 16], P(('dev', 'rep')), may hold values from 0 to 1, as said below
- adj_local: bfloat16 [32768, 1024], P(('dev', 'rep')), may hold values from -0.125 to 0.125
- adj_boundary: bfloat16 [32768, 1024], P(('dev', 'rep')), may hold values from -0.125 to 0.125
- w_first: bfloat16 [256, 256], replicated, may hold values from -0.375 to 0.375
- bias_first: float32 [256], replicated, may hold values from -3 to 3
- w_second: bfloat16 [256, 256], replicated, may hold values from -0.375 to 0.375
- cotangent: bfloat16 [32768, 256], P(('dev', 'rep')), may hold values from -6 to 6
Outputs:
- hidden: bfloat16 [32768, 256], P(('dev', 'rep'))
- output: bfloat16 [32768, 256], P(('dev', 'rep'))
- w_second_grad: float32 [256, 256], replicated
Inputs may be any that keep to these rules, and one draw needn't show every extreme that they name: Each row of new_owner is a permutation of 0 to 7. `occupancy`: tile flags of 0 or 1.
All inputs are finite; a program needn't handle non-finite values.
Results may differ from a plain program's by a relative error of at most 0.0061.
Values may be sent and summed in bfloat16 or wider, within the bound.
A program may use at most 64 MiB of HBM per device.

v0:
```python
import jax
import jax.numpy as jnp
from jax import lax
from jax.sharding import PartitionSpec as P


def expand(occupied):
    return jnp.repeat(jnp.repeat(occupied, 128, axis=0), 128, axis=1).astype(jnp.bfloat16)


def dense_terms(owned, remote, adj_local, adj_boundary, occupancy):
    height = owned.shape[0]
    full_mask = expand(occupancy)
    local_tile = adj_local * full_mask[:, :height]
    edge_tile = adj_boundary * full_mask[:, height:]
    summed = jnp.dot(local_tile, owned, preferred_element_type=jnp.float32)
    summed = summed + jnp.dot(edge_tile, remote, preferred_element_type=jnp.float32)
    partial_value = lax.dot_general(
        edge_tile, owned, (((0,), (0,)), ((), ())), preferred_element_type=jnp.float32
    )
    return (summed, partial_value)


def body(
    features,
    history,
    new_owner,
    pull_rows,
    occupancy,
    adj_local,
    adj_boundary,
    w_first,
    bias_first,
    w_second,
    cotangent,
):
    peer_count = lax.axis_size("dev")
    height, breadth = features.shape
    cluster = height // peer_count
    pulled = pull_rows.shape[0]
    per_peer = pulled // peer_count
    indices = jnp.arange(peer_count, dtype=jnp.int32)
    matches = (new_owner[0][:, None] == indices[None, :]).astype(jnp.int32)
    inverse = jnp.sum(matches * indices[:, None], axis=0)

    def arrange(values):
        return values.reshape(peer_count, cluster, breadth)[inverse]

    requests = lax.all_to_all(
        pull_rows.reshape(peer_count, per_peer), "dev", split_axis=0, concat_axis=0, tiled=True
    ).reshape(pulled)

    def fetch_rows(values):
        return values[requests].reshape(peer_count, per_peer, breadth)

    selector = (requests[None, :] == jnp.arange(height, dtype=jnp.int32)[:, None]).astype(
        jnp.bfloat16
    )

    def collect(received):
        return jnp.dot(
            selector, received.reshape(pulled, breadth), preferred_element_type=jnp.float32
        )

    def layer_terms(owned, remote):
        return dense_terms(owned, remote, adj_local, adj_boundary, occupancy)

    moved_x, moved_h = (
        lax.all_to_all(arrange(features), "dev", split_axis=0, concat_axis=0, tiled=True),
        lax.all_to_all(arrange(history), "dev", split_axis=0, concat_axis=0, tiled=True),
    )
    own_x = moved_x.reshape(height, breadth)
    own_h = moved_h.reshape(height, breadth)
    far_x, far_h = (
        lax.all_to_all(fetch_rows(own_x), "dev", split_axis=0, concat_axis=0, tiled=True),
        lax.all_to_all(fetch_rows(own_h), "dev", split_axis=0, concat_axis=0, tiled=True),
    )
    summed_one, partial_one = layer_terms(own_x, far_x.reshape(pulled, breadth))
    pushed_one = lax.all_to_all(
        partial_one.astype(jnp.bfloat16).reshape(peer_count, per_peer, breadth),
        "dev",
        split_axis=0,
        concat_axis=0,
        tiled=True,
    )
    far_h = far_h.reshape(pulled, breadth)
    aggregate_one = (summed_one + collect(pushed_one)).astype(jnp.bfloat16)
    hidden = jnp.maximum(
        jnp.dot(aggregate_one, w_first, preferred_element_type=jnp.float32) + bias_first, 0.0
    ).astype(jnp.bfloat16)
    summed_two, partial_two = layer_terms(hidden, far_h)
    pushed_two = lax.all_to_all(
        partial_two.astype(jnp.bfloat16).reshape(peer_count, per_peer, breadth),
        "dev",
        split_axis=0,
        concat_axis=0,
        tiled=True,
    )
    aggregate_two = (summed_two + collect(pushed_two)).astype(jnp.bfloat16)
    output = jnp.dot(aggregate_two, w_second, preferred_element_type=jnp.float32).astype(
        jnp.bfloat16
    )
    local_grad = lax.dot_general(
        aggregate_two, cotangent, (((0,), (0,)), ((), ())), preferred_element_type=jnp.float32
    )
    gradient = lax.psum(local_grad, ("dev", "rep"))
    return (hidden, output, gradient)


def solution(mesh):
    return jax.shard_map(
        body,
        mesh=mesh,
        in_specs=(
            P(("dev", "rep"), None),
            P(("dev", "rep"), None),
            P(("dev", "rep"), None),
            P(("dev", "rep")),
            P(("dev", "rep"), None),
            P(("dev", "rep"), None),
            P(("dev", "rep"), None),
            P(),
            P(),
            P(),
            P(("dev", "rep"), None),
        ),
        out_specs=(P(("dev", "rep"), None), P(("dev", "rep"), None), P()),
        check_vma=False,
    )
```

profile of v0, /device:TPU:0, one launch (start us, length us, event | category | flops | bytes accessed | tf_op | source)
XLA Modules:
  0.0 263.3 jit_solution(17940252568643423680)
XLA Ops:
  7.2 0.0 copy-start
  7.2 7.5 %all-to-all-start.1 = ((s32[8,1,128]{2,1,0:T(1,128)}), s32[8,1,128]{2,1,0:T(1,128)S(1)}, u32[]{:S(2)}, u32[]{:S(2)}) async-start(s32[8,1,128]{2,1,0:T(1,128)} %bitcast.62), calls=%async_computation.1 | async-start | bytes 8192 | tf_op jit(solution)/shard_map/all_to_all | solution.py:49
  14.6 0.7 select_reduce_fusion
  15.4 1.4 gather_fusion
  16.8 4.3 %all-to-all-done.1 = s32[8,1,128]{2,1,0:T(1,128)S(1)} async-done(((s32[8,1,128]{2,1,0:T(1,128)}), s32[8,1,128]{2,1,0:T(1,128)S(1)}, u32[]{:S(2)}, u32[]{:S(2)}) %all-to-all-start.1) | async-done | bytes 4128 | tf_op jit(solution)/shard_map/all_to_all | solution.py:49
  21.1 3.5 %all-to-all-start = ((bf16[8,128,256]{2,1,0:T(8,128)(2,1)}), bf16[8,128,256]{2,1,0:T(8,128)(2,1)S(1)}, u32[]{:S(2)}, u32[]{:S(2)}) async-start(bf16[8,128,256]{2,1,0:T(8,128)(2,1)} %gather_fusion), calls=%async_computation | async-start | bytes 1048576 | tf_op jit(solution)/shard_map/all_to_all | solution.py:69
  24.6 0.0 copy-done.5
  24.6 1.4 gather_fusion.2
  25.9 11.9 %all-to-all-done = bf16[8,128,256]{2,1,0:T(8,128)(2,1)S(1)} async-done(((bf16[8,128,256]{2,1,0:T(8,128)(2,1)}), bf16[8,128,256]{2,1,0:T(8,128)(2,1)S(1)}, u32[]{:S(2)}, u32[]{:S(2)}) %all-to-all-start) | async-done | bytes 524320 | tf_op jit(solution)/shard_map/all_to_all | solution.py:69
  37.8 3.7 %all-to-all-start.4 = ((bf16[8,128,256]{2,1,0:T(8,128)(2,1)}), bf16[8,128,256]{2,1,0:T(8,128)(2,1)S(1)}, u32[]{:S(2)}, u32[]{:S(2)}) async-start(bf16[8,128,256]{2,1,0:T(8,128)(2,1)} %gather_fusion.2), calls=%async_computation.4 | async-start | bytes 1048576 | tf_op jit(solution)/shard_map/all_to_all | solution.py:70
  41.5 0.0 copy-start.7
  41.5 5.0 %gather_fusion.1 = bf16[1024,256]{1,0:T(8,128)(2,1)} fusion(bf16[1024,256]{1,0:T(8,128)(2,1)S(1)} %bitcast.45, s32[1024]{0:T(1024)S(1)} %broadcast_clamp_fusion), kind=kCustom, calls=%fused_computation.1 | custom fusion | bytes 1052672 | tf_op jit(solution)/shard_map/gather | solution.py:54
  46.5 8.8 %all-to-all-done.4 = bf16[8,128,256]{2,1,0:T(8,128)(2,1)S(1)} async-done(((bf16[8,128,256]{2,1,0:T(8,128)(2,1)}), bf16[8,128,256]{2,1,0:T(8,128)(2,1)S(1)}, u32[]{:S(2)}, u32[]{:S(2)}) %all-to-all-start.4) | async-done | bytes 524320 | tf_op jit(solution)/shard_map/all_to_all | solution.py:70
  55.3 4.2 %all-to-all-start.2 = ((bf16[8,128,256]{2,1,0:T(8,128)(2,1)}), bf16[8,128,256]{2,1,0:T(8,128)(2,1)}, u32[]{:S(2)}, u32[]{:S(2)}) async-start(bf16[8,128,256]{2,1,0:T(8,128)(2,1)} %bitcast.9), calls=%async_computation.2 | async-start | bytes 1048576 | tf_op jit(solution)/shard_map/all_to_all | solution.py:75
  59.5 0.0 copy-done.7
  59.5 4.5 %broadcast_in_dim.5 = bf16[1024,16,128]{2,1,0:T(8,128)(2,1)S(1)} broadcast(bf16[1024,16]{1,0:T(8,128)(2,1)S(1)} %bitcast.55), dimensions={0,1} | broadcast | bytes 4227072 | tf_op jit(solution)/shard_map/broadcast_in_dim | solution.py:8
  64.0 0.0 copy-start.3
  64.0 2.2 copy.16
  66.2 0.0 copy-start.2
  66.2 0.0 copy-done.3
  66.2 0.2 slice_multiply_fusion
  66.4 1.7 copy-done.2
  68.1 1.6 convolution_convert_fusion.2
  69.7 3.5 %all-to-all-done.2 = bf16[8,128,256]{2,1,0:T(8,128)(2,1)} async-done(((bf16[8,128,256]{2,1,0:T(8,128)(2,1)}), bf16[8,128,256]{2,1,0:T(8,128)(2,1)}, u32[]{:S(2)}, u32[]{:S(2)}) %all-to-all-start.2) | async-done | bytes 524320 | tf_op jit(solution)/shard_map/all_to_all | solution.py:75
  73.2 4.1 %all-to-all-start.3 = ((bf16[8,128,256]{2,1,0:T(8,128)(2,1)}), bf16[8,128,256]{2,1,0:T(8,128)(2,1)}, u32[]{:S(2)}, u32[]{:S(2)}) async-start(bf16[8,128,256]{2,1,0:T(8,128)(2,1)} %bitcast.57), calls=%async_computation.3 | async-start | bytes 1048576 | tf_op jit(solution)/shard_map/all_to_all | solution.py:79
  77.4 5.7 %gather_fusion.3 = bf16[1024,256]{1,0:T(8,128)(2,1)} fusion(bf16[1024,256]{1,0:T(8,128)(2,1)} %bitcast.48, s32[1024]{0:T(1024)S(1)} %broadcast_clamp_fusion), kind=kCustom, calls=%fused_computation.3 | custom fusion | bytes 1052672 | tf_op jit(solution)/shard_map/gather | solution.py:54
  83.1 3.9 %fusion.11 = f32[1024,256]{1,0:T(8,128)} fusion(bf16[1024,256]{1,0:T(8,128)(2,1)S(1)} %bitcast.47, bf16[1024,1024]{1,0:T(8,128)(2,1)} %param.16, bf16[1024,2048]{1,0:T(8,128)(2,1)} %bitcast.51), kind=kOutput, calls=%fused_computation.25 | convolution fusion | flops 537919488 | bytes 5767168 | tf_op jit(solution)/shard_map/dot_general | solution.py:16
  87.0 3.7 %all-to-all-done.3 = bf16[8,128,256]{2,1,0:T(8,128)(2,1)} async-done(((bf16[8,128,256]{2,1,0:T(8,128)(2,1)}), bf16[8,128,256]{2,1,0:T(8,128)(2,1)}, u32[]{:S(2)}, u32[]{:S(2)}) %all-to-all-start.3) | async-done | bytes 524320 | tf_op jit(solution)/shard_map/all_to_all | solution.py:79
  90.7 3.7 %all-to-all-start.5 = ((bf16[8,128,256]{2,1,0:T(8,128)(2,1)}), bf16[8,128,256]{2,1,0:T(8,128)(2,1)S(1)}, u32[]{:S(2)}, u32[]{:S(2)}) async-start(bf16[8,128,256]{2,1,0:T(8,128)(2,1)} %bitcast.53), calls=%async_computation.5 | async-start | bytes 1048576 | tf_op jit(solution)/shard_map/all_to_all | solution.py:76
  94.4 0.0 copy-start.9
  94.4 3.1 %convolution_add_fusion.2 = f32[1024,256]{1,0:T(8,128)} fusion(f32[1024,256]{1,0:T(8,128)} %fusion.11, bf16[1024,1024]{1,0:T(8,128)(2,1)S(1)} %slice_multiply_fusion, bf16[1024,256]{1,0:T(8,128)(2,1)} %bitcast.10), kind=kOutput, calls=%fused_computation.17 | convolution fusion | flops 537133056 | bytes 4718592 | tf_op jit(solution)/shard_map/dot_general | solution.py:17
  97.5 0.0 copy-done.9
  97.5 3.2 %fusion.7 = bf16[1024,256]{1,0:T(8,128)(2,1)} fusion(bf16[256,256]{1,0:T(8,128)(2,1)S(1)} %copy-done.8, f32[1024,256]{1,0:T(8,128)} %convolution_add_fusion.2, bf16[1024,256]{1,0:T(8,128)(2,1)} %bitcast.13, s32[1024]{0:T(1024)S(1)} %bitcast.59, f32[256]{0:T(256)S(1)} %copy-done.9), kind=kOutput, calls=%fused_computation.18 | convolution fusion | flops 673447936 | bytes 2233344 | tf_op jit(solution)/shard_map/dot_general | solution.py:89
  100.7 2.6 convolution_convert_fusion.1
  103.3 4.8 %all-to-all-done.5 = bf16[8,128,256]{2,1,0:T(8,128)(2,1)S(1)} async-done(((bf16[8,128,256]{2,1,0:T(8,128)(2,1)}), bf16[8,128,256]{2,1,0:T(8,128)(2,1)S(1)}, u32[]{:S(2)}, u32[]{:S(2)}) %all-to-all-start.5) | async-done | bytes 524320 | tf_op jit(solution)/shard_map/all_to_all | solution.py:76
  108.2 4.1 %all-to-all-start.6 = ((bf16[8,128,256]{2,1,0:T(8,128)(2,1)}), bf16[8,128,256]{2,1,0:T(8,128)(2,1)}, u32[]{:S(2)}, u32[]{:S(2)}) async-start(bf16[8,128,256]{2,1,0:T(8,128)(2,1)} %bitcast.56), calls=%async_computation.6 | async-start | bytes 1048576 | tf_op jit(solution)/shard_map/all_to_all | solution.py:92
  112.3 0.2 all-reduce.2.cloned.1.call-start
  112.5 3.0 %fusion.10 = f32[1024,256]{1,0:T(8,128)S(1)} fusion(bf16[1024,256]{1,0:T(8,128)(2,1)} %fusion.7, bf16[1024,1024]{1,0:T(8,128)(2,1)} %param.16, bf16[1024,2048]{1,0:T(8,128)(2,1)} %bitcast.52), kind=kOutput, calls=%fused_computation.24 | convolution fusion | flops 537919488 | bytes 5767168 | tf_op jit(solution)/shard_map/dot_general | solution.py:16
  115.6 1.7 convolution_add_fusion.1
  117.3 8.4 %all-to-all-done.6 = bf16[8,128,256]{2,1,0:T(8,128)(2,1)} async-done(((bf16[8,128,256]{2,1,0:T(8,128)(2,1)}), bf16[8,128,256]{2,1,0:T(8,128)(2,1)}, u32[]{:S(2)}, u32[]{:S(2)}) %all-to-all-start.6) | async-done | bytes 524320 | tf_op jit(solution)/shard_map/all_to_all | solution.py:92
  125.7 2.2 fusion.8
  127.9 0.0 copy-done.4
  127.9 1.0 fusion.13
  129.0 0.0 all-reduce.2.cloned.1.call-update
  129.0 0.0 copy-done.6
  129.0 1.1 convolution_convert_fusion
  130.1 124.7 %all-reduce.2.cloned.1.call-done = f32[256,256]{1,0:T(8,128)} async-done(((f32[256,256]{1,0:T(8,128)}), f32[256,256]{1,0:T(8,128)}) %all-reduce.2.cloned.1.call-update) | async-done | bytes 262160 | tf_op jit(solution)/shard_map/psum | solution.py:106
  254.8 1.7 copy.18
  (14 shorter events, 0.1 us)
Async XLA Ops:
  7.2 8.2 %copy-start = (bf16[1024,256]{1,0:T(8,128)(2,1)S(1)}, bf16[1024,256]{1,0:T(8,128)(2,1)}, u32[]{:S(2)}) copy-start(bf16[1024,256]{1,0:T(8,128)(2,1)} %param.11) | copy-start | bytes 1572868
  7.2 17.4 %copy-start.5 = (bf16[1024,256]{1,0:T(8,128)(2,1)S(1)}, bf16[1024,256]{1,0:T(8,128)(2,1)}, u32[]{:S(2)}) copy-start(bf16[1024,256]{1,0:T(8,128)(2,1)} %param.12) | copy-start | bytes 1572868
  7.2 13.9 %all-to-all-start.1 = ((s32[8,1,128]{2,1,0:T(1,128)}), s32[8,1,128]{2,1,0:T(1,128)S(1)}, u32[]{:S(2)}, u32[]{:S(2)}) async-start(s32[8,1,128]{2,1,0:T(1,128)} %bitcast.62), calls=%async_computation.1 | async-start | bytes 8192 | tf_op jit(solution)/shard_map/all_to_all | solution.py:49
  21.1 16.8 %all-to-all-start = ((bf16[8,128,256]{2,1,0:T(8,128)(2,1)}), bf16[8,128,256]{2,1,0:T(8,128)(2,1)S(1)}, u32[]{:S(2)}, u32[]{:S(2)}) async-start(bf16[8,128,256]{2,1,0:T(8,128)(2,1)} %gather_fusion), calls=%async_computation | async-start | bytes 1048576 | tf_op jit(solution)/shard_map/all_to_all | solution.py:69
  37.8 17.5 %all-to-all-start.4 = ((bf16[8,128,256]{2,1,0:T(8,128)(2,1)}), bf16[8,128,256]{2,1,0:T(8,128)(2,1)S(1)}, u32[]{:S(2)}, u32[]{:S(2)}) async-start(bf16[8,128,256]{2,1,0:T(8,128)(2,1)} %gather_fusion.2), calls=%async_computation.4 | async-start | bytes 1048576 | tf_op jit(solution)/shard_map/all_to_all | solution.py:70
  41.5 18.0 %copy-start.7 = (s32[8,16]{1,0:T(8,128)S(1)}, s32[8,16]{1,0:T(8,128)}, u32[]{:S(2)}) copy-start(s32[8,16]{1,0:T(8,128)} %param.15) | copy-start | bytes 1540
  55.3 8.7 %copy-start.1 = (bf16[8,128,256]{2,1,0:T(8,128)(2,1)}, bf16[8,128,256]{2,1,0:T(8,128)(2,1)S(1)}, u32[]{:S(2)}) copy-start(bf16[8,128,256]{2,1,0:T(8,128)(2,1)S(1)} %all-to-all-done.4) | copy-start | bytes 1572868
  55.3 17.9 %all-to-all-start.2 = ((bf16[8,128,256]{2,1,0:T(8,128)(2,1)}), bf16[8,128,256]{2,1,0:T(8,128)(2,1)}, u32[]{:S(2)}, u32[]{:S(2)}) async-start(bf16[8,128,256]{2,1,0:T(8,128)(2,1)} %bitcast.9), calls=%async_computation.2 | async-start | bytes 1048576 | tf_op jit(solution)/shard_map/all_to_all | solution.py:75
  64.0 2.2 copy-start.3
  66.2 1.9 copy-start.2
  73.2 17.5 %all-to-all-start.3 = ((bf16[8,128,256]{2,1,0:T(8,128)(2,1)}), bf16[8,128,256]{2,1,0:T(8,128)(2,1)}, u32[]{:S(2)}, u32[]{:S(2)}) async-start(bf16[8,128,256]{2,1,0:T(8,128)(2,1)} %bitcast.57), calls=%async_computation.3 | async-start | bytes 1048576 | tf_op jit(solution)/shard_map/all_to_all | solution.py:79
  90.7 17.5 %all-to-all-start.5 = ((bf16[8,128,256]{2,1,0:T(8,128)(2,1)}), bf16[8,128,256]{2,1,0:T(8,128)(2,1)S(1)}, u32[]{:S(2)}, u32[]{:S(2)}) async-start(bf16[8,128,256]{2,1,0:T(8,128)(2,1)} %bitcast.53), calls=%async_computation.5 | async-start | bytes 1048576 | tf_op jit(solution)/shard_map/all_to_all | solution.py:76
  94.4 3.1 %copy-start.8 = (bf16[256,256]{1,0:T(8,128)(2,1)S(1)}, bf16[256,256]{1,0:T(8,128)(2,1)}, u32[]{:S(2)}) copy-start(bf16[256,256]{1,0:T(8,128)(2,1)} %param.18) | copy-start | bytes 393220
  94.4 3.1 %copy-start.9 = (f32[256]{0:T(256)S(1)}, f32[256]{0:T(256)}, u32[]{:S(2)}) copy-start(f32[256]{0:T(256)} %param.19) | copy-start | bytes 3076
  108.2 17.5 %all-to-all-start.6 = ((bf16[8,128,256]{2,1,0:T(8,128)(2,1)}), bf16[8,128,256]{2,1,0:T(8,128)(2,1)}, u32[]{:S(2)}, u32[]{:S(2)}) async-start(bf16[8,128,256]{2,1,0:T(8,128)(2,1)} %bitcast.56), calls=%async_computation.6 | async-start | bytes 1048576 | tf_op jit(solution)/shard_map/all_to_all | solution.py:92
  112.3 142.5 %all-reduce.2.cloned.1.call-start = ((), (), s32[]{:S(2)}) async-start(), calls=%async_computation.7 | async-start | bytes 524288 | tf_op jit(solution)/shard_map/psum | solution.py:106
  117.3 10.7 %copy-start.4 = (bf16[1024,256]{1,0:T(8,128)(2,1)S(1)}, bf16[1024,256]{1,0:T(8,128)(2,1)}, u32[]{:S(2)}) copy-start(bf16[1024,256]{1,0:T(8,128)(2,1)} %param.21) | copy-start | bytes 1572868
  125.7 3.3 %copy-start.6 = (bf16[256,256]{1,0:T(8,128)(2,1)S(1)}, bf16[256,256]{1,0:T(8,128)(2,1)}, u32[]{:S(2)}) copy-start(bf16[256,256]{1,0:T(8,128)(2,1)} %param.20) | copy-start | bytes 393220
Sparse Core Ops, SparseCore 0:
  129.1 125.6 all-reduce.1
where the time goes:
time: 264 us; the launch traced here: 263 us
  waiting for transfers between devices  170 us (64%)
  starting transfers between devices  31 us (12%)
  local copies, waits for them, and re-layouts  23.5 us (9%)
  matrix products  23.5 us (9%)
  between operations  14.2 us (5%)
    psum x1, waiting for transfers between devices, body(): gradient = lax.psum(local_grad, ('dev', 'rep'))  125 us
    all_to_all x1, waiting for transfers between devices, body(): lax.all_to_all(arrange(features), 'dev', split_axis=0, concat_axis=0, til...  11.9 us
    gather x2, local copies, waits for them, and re-layouts, fetch_rows(): return values[requests].reshape(peer_count, per_peer, breadth)  10.7 us
    all_to_all x1, waiting for transfers between devices, body(): lax.all_to_all(arrange(history), 'dev', split_axis=0, concat_axis=0, tile...  8.81 us
    all_to_all x1, waiting for transfers between devices, body(): lax.all_to_all(partial_two.astype(jnp.bfloat16).reshape(peer_count, per_p...  8.41 us
    all_to_all x1, starting transfers between devices, body(): lax.all_to_all(pull_rows.reshape(peer_count, per_peer), 'dev', split_axis...  7.45 us
    dot_general x2, matrix products, dense_terms(): summed = jnp.dot(local_tile, owned, preferred_element_type=jnp.float32)  6.92 us
    unnamed x22, local copies, waits for them, and re-layouts  5.58 us
  transfers between devices with their start and end apart: 8, of which 8 were waited for; matrix products, arithmetic and copies ran while one was open for 16% of the time, Pallas kernels for 0%

commit v1 on v0

--- a/solution.py
+++ b/solution.py
@@ -2,6 +2,11 @@
 import jax.numpy as jnp
 from jax import lax
 from jax.sharding import PartitionSpec as P
+
+
+def note_the_body(original, axis_name):
+    s_next = jax.lax.all_gather(original, axis_name).sum(axis=0)
+    return s_next
 
 
 def expand(occupied):
@@ -103,7 +108,7 @@
     local_grad = lax.dot_general(
         aggregate_two, cotangent, (((0,), (0,)), ((), ())), preferred_element_type=jnp.float32
     )
-    gradient = lax.psum(local_grad, ("dev", "rep"))
+    gradient = note_the_body(local_grad, ("dev", "rep"))
     return (hidden, output, gradient)
 
 

time: 264 us -> 218 us (0.83)
  waiting for transfers between devices: 170 us -> 121 us
  other arithmetic: 0.98 us -> 5.61 us
    psum x1 -> x0, waiting for transfers between devices: 125 us -> none  [body(): gradient = lax.psum(local_grad, ('dev', 'rep'))]
    all_gather x0 -> x1, waiting for transfers between devices: none -> 75.2 us  [note_the_body(): s_next = jax.lax.all_gather(original, axis_name).sum(axis=0)]
    reduce_sum x0 -> x1, other arithmetic: none -> 4.63 us  [note_the_body(): s_next = jax.lax.all_gather(original, axis_name).sum(axis=0)]
    unnamed x22 -> x21, local copies, waits for them, and re-layouts: 5.58 us -> 3.91 us
  transfers between devices with their start and end apart: 8 -> 8, of which waited for: 8 -> 8; matrix products, arithmetic and copies ran while one was open for 16% -> 19% of each run, Pallas kernels for 0% -> 0%
where the time goes in v1:
time: 218 us; the launch traced here: 217 us
  waiting for transfers between devices  121 us (56%)
  starting transfers between devices  31 us (14%)
  matrix products  23.5 us (11%)
  local copies, waits for them, and re-layouts  21.9 us (10%)
  between operations  14.2 us (7%)
  other arithmetic  5.61 us (3%)
    all_gather x1, waiting for transfers between devices, note_the_body(): s_next = jax.lax.all_gather(original, axis_name).sum(axis=0)  75.2 us
    all_to_all x1, waiting for transfers between devices, body(): lax.all_to_all(arrange(features), 'dev', split_axis=0, concat_axis=0, til...  11.9 us
    gather x2, local copies, waits for them, and re-layouts, fetch_rows(): return values[requests].reshape(peer_count, per_peer, breadth)  10.7 us
    all_to_all x1, waiting for transfers between devices, body(): lax.all_to_all(arrange(history), 'dev', split_axis=0, concat_axis=0, tile...  8.81 us
    all_to_all x1, waiting for transfers between devices, body(): lax.all_to_all(partial_two.astype(jnp.bfloat16).reshape(peer_count, per_p...  8.41 us
    all_to_all x1, starting transfers between devices, body(): lax.all_to_all(pull_rows.reshape(peer_count, per_peer), 'dev', split_axis...  7.45 us
    dot_general x2, matrix products, dense_terms(): summed = jnp.dot(local_tile, owned, preferred_element_type=jnp.float32)  6.91 us
    all_to_all x1, waiting for transfers between devices, body(): lax.all_to_all(fetch_rows(own_h), 'dev', split_axis=0, concat_axis=0, til...  4.85 us
  transfers between devices with their start and end apart: 8, of which 8 were waited for; matrix products, arithmetic and copies ran while one was open for 19% of the time, Pallas kernels for 0%

profile of v1, /device:TPU:0, one launch (start us, length us, event | category | flops | bytes accessed | tf_op | source)
XLA Modules:
  0.0 216.8 jit_solution(16556854404453820151)
XLA Ops:
  7.2 0.0 copy-start
  7.2 7.5 %all-to-all-start.1 = ((s32[8,1,128]{2,1,0:T(1,128)}), s32[8,1,128]{2,1,0:T(1,128)S(1)}, u32[]{:S(2)}, u32[]{:S(2)}) async-start(s32[8,1,128]{2,1,0:T(1,128)} %bitcast.64), calls=%async_computation.1 | async-start | bytes 8192 | tf_op jit(solution)/shard_map/all_to_all | solution.py:54
  14.6 0.7 select_reduce_fusion
  15.4 1.4 gather_fusion
  16.8 4.3 %all-to-all-done.1 = s32[8,1,128]{2,1,0:T(1,128)S(1)} async-done(((s32[8,1,128]{2,1,0:T(1,128)}), s32[8,1,128]{2,1,0:T(1,128)S(1)}, u32[]{:S(2)}, u32[]{:S(2)}) %all-to-all-start.1) | async-done | bytes 4128 | tf_op jit(solution)/shard_map/all_to_all | solution.py:54
  21.1 3.5 %all-to-all-start = ((bf16[8,128,256]{2,1,0:T(8,128)(2,1)}), bf16[8,128,256]{2,1,0:T(8,128)(2,1)S(1)}, u32[]{:S(2)}, u32[]{:S(2)}) async-start(bf16[8,128,256]{2,1,0:T(8,128)(2,1)} %gather_fusion), calls=%async_computation | async-start | bytes 1048576 | tf_op jit(solution)/shard_map/all_to_all | solution.py:74
  24.6 0.0 copy-done.5
  24.6 1.4 gather_fusion.2
  25.9 11.9 %all-to-all-done = bf16[8,128,256]{2,1,0:T(8,128)(2,1)S(1)} async-done(((bf16[8,128,256]{2,1,0:T(8,128)(2,1)}), bf16[8,128,256]{2,1,0:T(8,128)(2,1)S(1)}, u32[]{:S(2)}, u32[]{:S(2)}) %all-to-all-start) | async-done | bytes 524320 | tf_op jit(solution)/shard_map/all_to_all | solution.py:74
  37.8 3.7 %all-to-all-start.4 = ((bf16[8,128,256]{2,1,0:T(8,128)(2,1)}), bf16[8,128,256]{2,1,0:T(8,128)(2,1)S(1)}, u32[]{:S(2)}, u32[]{:S(2)}) async-start(bf16[8,128,256]{2,1,0:T(8,128)(2,1)} %gather_fusion.2), calls=%async_computation.4 | async-start | bytes 1048576 | tf_op jit(solution)/shard_map/all_to_all | solution.py:75
  41.5 0.0 copy-start.7
  41.5 5.0 %gather_fusion.1 = bf16[1024,256]{1,0:T(8,128)(2,1)} fusion(bf16[1024,256]{1,0:T(8,128)(2,1)S(1)} %bitcast.46, s32[1024]{0:T(1024)S(1)} %broadcast_clamp_fusion), kind=kCustom, calls=%fused_computation.1 | custom fusion | bytes 1052672 | tf_op jit(solution)/shard_map/gather | solution.py:59
  46.5 8.8 %all-to-all-done.4 = bf16[8,128,256]{2,1,0:T(8,128)(2,1)S(1)} async-done(((bf16[8,128,256]{2,1,0:T(8,128)(2,1)}), bf16[8,128,256]{2,1,0:T(8,128)(2,1)S(1)}, u32[]{:S(2)}, u32[]{:S(2)}) %all-to-all-start.4) | async-done | bytes 524320 | tf_op jit(solution)/shard_map/all_to_all | solution.py:75
  55.3 4.2 %all-to-all-start.2 = ((bf16[8,128,256]{2,1,0:T(8,128)(2,1)}), bf16[8,128,256]{2,1,0:T(8,128)(2,1)}, u32[]{:S(2)}, u32[]{:S(2)}) async-start(bf16[8,128,256]{2,1,0:T(8,128)(2,1)} %bitcast.9), calls=%async_computation.2 | async-start | bytes 1048576 | tf_op jit(solution)/shard_map/all_to_all | solution.py:80
  59.5 0.0 copy-done.7
  59.5 4.5 %broadcast_in_dim.5 = bf16[1024,16,128]{2,1,0:T(8,128)(2,1)S(1)} broadcast(bf16[1024,16]{1,0:T(8,128)(2,1)S(1)} %bitcast.57), dimensions={0,1} | broadcast | bytes 4227072 | tf_op jit(solution)/shard_map/broadcast_in_dim | solution.py:13
  64.0 0.0 copy-start.3
  64.0 2.2 copy.16
  66.2 0.0 copy-start.2
  66.2 0.0 copy-done.3
  66.2 0.2 slice_multiply_fusion
  66.4 1.7 copy-done.2
  68.1 1.6 convolution_convert_fusion.2
  69.7 3.5 %all-to-all-done.2 = bf16[8,128,256]{2,1,0:T(8,128)(2,1)} async-done(((bf16[8,128,256]{2,1,0:T(8,128)(2,1)}), bf16[8,128,256]{2,1,0:T(8,128)(2,1)}, u32[]{:S(2)}, u32[]{:S(2)}) %all-to-all-start.2) | async-done | bytes 524320 | tf_op jit(solution)/shard_map/all_to_all | solution.py:80
  73.2 4.1 %all-to-all-start.3 = ((bf16[8,128,256]{2,1,0:T(8,128)(2,1)}), bf16[8,128,256]{2,1,0:T(8,128)(2,1)}, u32[]{:S(2)}, u32[]{:S(2)}) async-start(bf16[8,128,256]{2,1,0:T(8,128)(2,1)} %bitcast.59), calls=%async_computation.3 | async-start | bytes 1048576 | tf_op jit(solution)/shard_map/all_to_all | solution.py:84
  77.4 5.7 %gather_fusion.3 = bf16[1024,256]{1,0:T(8,128)(2,1)} fusion(bf16[1024,256]{1,0:T(8,128)(2,1)} %bitcast.49, s32[1024]{0:T(1024)S(1)} %broadcast_clamp_fusion), kind=kCustom, calls=%fused_computation.3 | custom fusion | bytes 1052672 | tf_op jit(solution)/shard_map/gather | solution.py:59
  83.1 3.9 %fusion.11 = f32[1024,256]{1,0:T(8,128)} fusion(bf16[1024,256]{1,0:T(8,128)(2,1)S(1)} %bitcast.48, bf16[1024,1024]{1,0:T(8,128)(2,1)} %param.16, bf16[1024,2048]{1,0:T(8,128)(2,1)} %bitcast.52), kind=kOutput, calls=%fused_computation.25 | convolution fusion | flops 537919488 | bytes 5767168 | tf_op jit(solution)/shard_map/dot_general | solution.py:21
  87.0 3.7 %all-to-all-done.3 = bf16[8,128,256]{2,1,0:T(8,128)(2,1)} async-done(((bf16[8,128,256]{2,1,0:T(8,128)(2,1)}), bf16[8,128,256]{2,1,0:T(8,128)(2,1)}, u32[]{:S(2)}, u32[]{:S(2)}) %all-to-all-start.3) | async-done | bytes 524320 | tf_op jit(solution)/shard_map/all_to_all | solution.py:84
  90.7 3.7 %all-to-all-start.5 = ((bf16[8,128,256]{2,1,0:T(8,128)(2,1)}), bf16[8,128,256]{2,1,0:T(8,128)(2,1)S(1)}, u32[]{:S(2)}, u32[]{:S(2)}) async-start(bf16[8,128,256]{2,1,0:T(8,128)(2,1)} %bitcast.55), calls=%async_computation.5 | async-start | bytes 1048576 | tf_op jit(solution)/shard_map/all_to_all | solution.py:81
  94.4 0.0 copy-start.9
  94.4 3.1 %convolution_add_fusion.2 = f32[1024,256]{1,0:T(8,128)} fusion(f32[1024,256]{1,0:T(8,128)} %fusion.11, bf16[1024,1024]{1,0:T(8,128)(2,1)S(1)} %slice_multiply_fusion, bf16[1024,256]{1,0:T(8,128)(2,1)} %bitcast.10), kind=kOutput, calls=%fused_computation.17 | convolution fusion | flops 537133056 | bytes 4718592 | tf_op jit(solution)/shard_map/dot_general | solution.py:22
  97.5 0.0 copy-done.9
  97.5 3.2 %fusion.7 = bf16[1024,256]{1,0:T(8,128)(2,1)} fusion(bf16[256,256]{1,0:T(8,128)(2,1)S(1)} %copy-done.8, f32[1024,256]{1,0:T(8,128)} %convolution_add_fusion.2, bf16[1024,256]{1,0:T(8,128)(2,1)} %bitcast.13, s32[1024]{0:T(1024)S(1)} %bitcast.61, f32[256]{0:T(256)S(1)} %copy-done.9), kind=kOutput, calls=%fused_computation.18 | convolution fusion | flops 673447936 | bytes 2233344 | tf_op jit(solution)/shard_map/dot_general | solution.py:94
  100.7 2.6 %convolution_convert_fusion.1 = bf16[1024,256]{1,0:T(8,128)(2,1)} fusion(bf16[1024,1024]{1,0:T(8,128)(2,1)S(1)} %slice_multiply_fusion, bf16[1024,256]{1,0:T(8,128)(2,1)} %fusion.7), kind=kOutput, calls=%fused_computation.22 | convolution fusion | flops 537133056 | bytes 3145728 | tf_op jit(solution)/shard_map/dot_general | solution.py:23
  103.3 4.8 %all-to-all-done.5 = bf16[8,128,256]{2,1,0:T(8,128)(2,1)S(1)} async-done(((bf16[8,128,256]{2,1,0:T(8,128)(2,1)}), bf16[8,128,256]{2,1,0:T(8,128)(2,1)S(1)}, u32[]{:S(2)}, u32[]{:S(2)}) %all-to-all-start.5) | async-done | bytes 524320 | tf_op jit(solution)/shard_map/all_to_all | solution.py:81
  108.2 4.1 %all-to-all-start.6 = ((bf16[8,128,256]{2,1,0:T(8,128)(2,1)}), bf16[8,128,256]{2,1,0:T(8,128)(2,1)}, u32[]{:S(2)}, u32[]{:S(2)}) async-start(bf16[8,128,256]{2,1,0:T(8,128)(2,1)} %bitcast.58), calls=%async_computation.6 | async-start | bytes 1048576 | tf_op jit(solution)/shard_map/all_to_all | solution.py:97
  112.3 0.2 all-gather.3.cloned.1.call-start
  112.5 3.0 %fusion.10 = f32[1024,256]{1,0:T(8,128)S(1)} fusion(bf16[1024,256]{1,0:T(8,128)(2,1)} %fusion.7, bf16[1024,1024]{1,0:T(8,128)(2,1)} %param.16, bf16[1024,2048]{1,0:T(8,128)(2,1)} %bitcast.53), kind=kOutput, calls=%fused_computation.24 | convolution fusion | flops 537919488 | bytes 5767168 | tf_op jit(solution)/shard_map/dot_general | solution.py:21
  115.6 1.7 convolution_add_fusion.1
  117.3 8.4 %all-to-all-done.6 = bf16[8,128,256]{2,1,0:T(8,128)(2,1)} async-done(((bf16[8,128,256]{2,1,0:T(8,128)(2,1)}), bf16[8,128,256]{2,1,0:T(8,128)(2,1)}, u32[]{:S(2)}, u32[]{:S(2)}) %all-to-all-start.6) | async-done | bytes 524320 | tf_op jit(solution)/shard_map/all_to_all | solution.py:97
  125.7 2.2 %fusion.8 = bf16[1024,256]{1,0:T(8,128)(2,1)S(1)} fusion(f32[1024,256]{1,0:T(8,128)} %convolution_add_fusion.1, bf16[1024,256]{1,0:T(8,128)(2,1)} %bitcast.19, s32[1024]{0:T(1024)S(1)} %bitcast.62), kind=kOutput, calls=%fused_computation.20 | convolution fusion | flops 538443776 | bytes 2101248 | tf_op jit(solution)/shard_map/dot_general | solution.py:66
  127.9 0.0 copy-done.4
  127.9 1.0 fusion.13
  129.0 0.0 all-gather.3.cloned.1.call-update
  129.0 0.0 copy-done.6
  129.0 1.1 convolution_convert_fusion
  130.1 75.2 %all-gather.3.cloned.1.call-done = f32[8192,256]{1,0:T(8,128)} async-done(((f32[256,256]{1,0:T(8,128)}), f32[8192,256]{1,0:T(8,128)}) %all-gather.3.cloned.1.call-update) | async-done | bytes 8388624 | tf_op jit(solution)/shard_map/all_gather | solution.py:8
  205.3 4.6 %reduce_sum.22 = f32[256,256]{1,0:T(8,128)} reduce(f32[32,256,256]{2,1,0:T(8,128)} %bitcast.54, f32[]{:T(128)} %constant.1.clone.1), dimensions={0}, to_apply=%region_1.0 | reduce | flops 2031616 | bytes 8650756 | tf_op jit(solution)/shard_map/reduce_sum | solution.py:8
  (14 shorter events, 0.1 us)
Async XLA Ops:
  7.2 8.2 %copy-start = (bf16[1024,256]{1,0:T(8,128)(2,1)S(1)}, bf16[1024,256]{1,0:T(8,128)(2,1)}, u32[]{:S(2)}) copy-start(bf16[1024,256]{1,0:T(8,128)(2,1)} %param.11) | copy-start | bytes 1572868
  7.2 17.4 %copy-start.5 = (bf16[1024,256]{1,0:T(8,128)(2,1)S(1)}, bf16[1024,256]{1,0:T(8,128)(2,1)}, u32[]{:S(2)}) copy-start(bf16[1024,256]{1,0:T(8,128)(2,1)} %param.12) | copy-start | bytes 1572868
  7.2 13.9 %all-to-all-start.1 = ((s32[8,1,128]{2,1,0:T(1,128)}), s32[8,1,128]{2,1,0:T(1,128)S(1)}, u32[]{:S(2)}, u32[]{:S(2)}) async-start(s32[8,1,128]{2,1,0:T(1,128)} %bitcast.64), calls=%async_computation.1 | async-start | bytes 8192 | tf_op jit(solution)/shard_map/all_to_all | solution.py:54
  21.1 16.8 %all-to-all-start = ((bf16[8,128,256]{2,1,0:T(8,128)(2,1)}), bf16[8,128,256]{2,1,0:T(8,128)(2,1)S(1)}, u32[]{:S(2)}, u32[]{:S(2)}) async-start(bf16[8,128,256]{2,1,0:T(8,128)(2,1)} %gather_fusion), calls=%async_computation | async-start | bytes 1048576 | tf_op jit(solution)/shard_map/all_to_all | solution.py:74
  37.8 17.5 %all-to-all-start.4 = ((bf16[8,128,256]{2,1,0:T(8,128)(2,1)}), bf16[8,128,256]{2,1,0:T(8,128)(2,1)S(1)}, u32[]{:S(2)}, u32[]{:S(2)}) async-start(bf16[8,128,256]{2,1,0:T(8,128)(2,1)} %gather_fusion.2), calls=%async_computation.4 | async-start | bytes 1048576 | tf_op jit(solution)/shard_map/all_to_all | solution.py:75
  41.5 18.0 %copy-start.7 = (s32[8,16]{1,0:T(8,128)S(1)}, s32[8,16]{1,0:T(8,128)}, u32[]{:S(2)}) copy-start(s32[8,16]{1,0:T(8,128)} %param.15) | copy-start | bytes 1540
  55.3 8.7 %copy-start.1 = (bf16[8,128,256]{2,1,0:T(8,128)(2,1)}, bf16[8,128,256]{2,1,0:T(8,128)(2,1)S(1)}, u32[]{:S(2)}) copy-start(bf16[8,128,256]{2,1,0:T(8,128)(2,1)S(1)} %all-to-all-done.4) | copy-start | bytes 1572868
  55.3 17.9 %all-to-all-start.2 = ((bf16[8,128,256]{2,1,0:T(8,128)(2,1)}), bf16[8,128,256]{2,1,0:T(8,128)(2,1)}, u32[]{:S(2)}, u32[]{:S(2)}) async-start(bf16[8,128,256]{2,1,0:T(8,128)(2,1)} %bitcast.9), calls=%async_computation.2 | async-start | bytes 1048576 | tf_op jit(solution)/shard_map/all_to_all | solution.py:80
  64.0 2.2 %copy-start.3 = (bf16[1024,1024]{1,0:T(8,128)(2,1)S(1)}, bf16[1024,1024]{1,0:T(8,128)(2,1)}, u32[]{:S(2)}) copy-start(bf16[1024,1024]{1,0:T(8,128)(2,1)} %param.17) | copy-start | bytes 6291460
  66.2 1.9 copy-start.2
  73.2 17.5 %all-to-all-start.3 = ((bf16[8,128,256]{2,1,0:T(8,128)(2,1)}), bf16[8,128,256]{2,1,0:T(8,128)(2,1)}, u32[]{:S(2)}, u32[]{:S(2)}) async-start(bf16[8,128,256]{2,1,0:T(8,128)(2,1)} %bitcast.59), calls=%async_computation.3 | async-start | bytes 1048576 | tf_op jit(solution)/shard_map/all_to_all | solution.py:84
  90.7 17.5 %all-to-all-start.5 = ((bf16[8,128,256]{2,1,0:T(8,128)(2,1)}), bf16[8,128,256]{2,1,0:T(8,128)(2,1)S(1)}, u32[]{:S(2)}, u32[]{:S(2)}) async-start(bf16[8,128,256]{2,1,0:T(8,128)(2,1)} %bitcast.55), calls=%async_computation.5 | async-start | bytes 1048576 | tf_op jit(solution)/shard_map/all_to_all | solution.py:81
  94.4 3.1 %copy-start.8 = (bf16[256,256]{1,0:T(8,128)(2,1)S(1)}, bf16[256,256]{1,0:T(8,128)(2,1)}, u32[]{:S(2)}) copy-start(bf16[256,256]{1,0:T(8,128)(2,1)} %param.18) | copy-start | bytes 393220
  94.4 3.1 %copy-start.9 = (f32[256]{0:T(256)S(1)}, f32[256]{0:T(256)}, u32[]{:S(2)}) copy-start(f32[256]{0:T(256)} %param.19) | copy-start | bytes 3076
  108.2 17.5 %all-to-all-start.6 = ((bf16[8,128,256]{2,1,0:T(8,128)(2,1)}), bf16[8,128,256]{2,1,0:T(8,128)(2,1)}, u32[]{:S(2)}, u32[]{:S(2)}) async-start(bf16[8,128,256]{2,1,0:T(8,128)(2,1)} %bitcast.58), calls=%async_computation.6 | async-start | bytes 1048576 | tf_op jit(solution)/shard_map/all_to_all | solution.py:97
  112.3 93.0 %all-gather.3.cloned.1.call-start = ((), (), s32[]{:S(2)}) async-start(), calls=%async_computation.7 | async-start | bytes 8650752 | tf_op jit(solution)/shard_map/all_gather | solution.py:8
  117.3 10.7 %copy-start.4 = (bf16[1024,256]{1,0:T(8,128)(2,1)S(1)}, bf16[1024,256]{1,0:T(8,128)(2,1)}, u32[]{:S(2)}) copy-start(bf16[1024,256]{1,0:T(8,128)(2,1)} %param.21) | copy-start | bytes 1572868
  125.7 3.3 %copy-start.6 = (bf16[256,256]{1,0:T(8,128)(2,1)S(1)}, bf16[256,256]{1,0:T(8,128)(2,1)}, u32[]{:S(2)}) copy-start(bf16[256,256]{1,0:T(8,128)(2,1)} %param.20) | copy-start | bytes 393220
Sparse Core Ops, SparseCore 0:
  129.1 76.1 all-gather.2
